TPU v7x, 8 devices: a whole 2x2x1 slice. The times are simulated.
8 devices in a mesh: dp: 2 (over z, y), tp: 4 (over x, core).
Axes of the slice: x: 2, y: 2, z: 1, core: 2. Of those that a mesh axis runs over, the one named last changes fastest.
Arguments:
- tokens: bfloat16 [512, 512], P('dp'), parts along dimension 0
- seq_lens: int32 [512], P('dp'), parts along dimension 0
- k_cache: bfloat16 [2, 512, 76, 8, 64], P(None, 'dp', None, 'tp'), parts along dimension 1
- v_cache: bfloat16 [2, 512, 76, 8, 64], P(None, 'dp', None, 'tp'), parts along dimension 1
- mem_k: bfloat16 [2, 512, 256, 8, 64], P(None, 'dp', None, 'tp'), parts along dimension 1
- mem_v: bfloat16 [2, 512, 256, 8, 64], P(None, 'dp', None, 'tp'), parts along dimension 1
- ln_attn: float32 [2, 2, 512], replicated
- w_qkv: bfloat16 [2, 512, 3, 512], P(None, None, None, 'tp')
- b_qkv: float32 [2, 3, 512], P(None, None, 'tp')
- w_o: bfloat16 [2, 512, 512], P(None, 'tp')
- b_o: float32 [2, 512], replicated
- ln_cross: float32 [2, 2, 512], replicated
- w_qc: bfloat16 [2, 512, 512], P(None, None, 'tp')
- b_qc: float32 [2, 512], P(None, 'tp')
- w_oc: bfloat16 [2, 512, 512], P(None, 'tp')
- b_oc: float32 [2, 512], replicated
- ln_mlp: float32 [2, 2, 512], replicated
- w_fc1: bfloat16 [2, 512, 2048], P(None, None, 'tp')
- b_fc1: float32 [2, 2048], P(None, 'tp')
- w_fc2: bfloat16 [2, 2048, 512], P(None, 'tp')
- b_fc2: float32 [2, 512], replicated
- ln_final: float32 [2, 512], replicated
- w_out: bfloat16 [512, 49408], P(None, 'tp')
Outputs:
- output 1: float32 [512, 49408], P('dp', 'tp'), parts along dimension 0
- output 2: bfloat16 [2, 512, 76, 8, 64], P(None, 'dp', None, 'tp'), parts along dimension 1
- output 3: bfloat16 [2, 512, 76, 8, 64], P(None, 'dp', None, 'tp'), parts along dimension 1
There are 2 independent parts. A program takes and returns all parts, laid end to end along the dimension named above; an argument that names none is the same for every part.
All inputs are finite; a program needn't handle non-finite values.
Results may differ from a plain program's by a relative error of at most 0.00401784.
Values are sent between devices in bfloat16 or wider.
A program may use at most 1 GiB of HBM per device.

v0:
```python
import jax
import jax.numpy as jnp
from jax import lax
from jax.sharding import PartitionSpec as P


def layer_norm(hidden, params):
    mean_val = jnp.mean(hidden, axis=-1, keepdims=True)
    centred = hidden - mean_val
    variance = jnp.mean(centred * centred, axis=-1, keepdims=True)
    return (centred * lax.rsqrt(variance + 1e-5) * params[0] + params[1]).astype(jnp.bfloat16)


def attend(query_heads, key_heads, value_heads, keep_mask):
    scores = jnp.einsum('bhd,bjhd->bhj', query_heads, key_heads, preferred_element_type=jnp.float32) * query_heads.shape[-1] ** -0.5
    scores = jnp.where(keep_mask, scores, -1e30)
    attn_probs = jax.nn.softmax(scores, axis=-1).astype(jnp.bfloat16)
    mixed_vals = jnp.einsum('bhj,bjhd->bhd', attn_probs, value_heads, preferred_element_type=jnp.float32).astype(jnp.bfloat16)
    return mixed_vals.reshape(mixed_vals.shape[0], -1)


def solution(mesh):
    cache_spec = P(None, 'dp', None, 'tp', None)
    in_specs = (P('dp', None), P('dp'), cache_spec, cache_spec, cache_spec, cache_spec,
                P(), P(None, None, None, 'tp'), P(None, None, 'tp'), P(None, 'tp', None), P(),
                P(), P(None, None, 'tp'), P(None, 'tp'), P(None, 'tp', None), P(),
                P(), P(None, None, 'tp'), P(None, 'tp'), P(None, 'tp', None), P(),
                P(), P(None, 'tp'))
    out_specs = (P('dp', 'tp'), cache_spec, cache_spec)

    def local_step(tokens, seq_lens, k_cache, v_cache, mem_k, mem_v, ln_attn, w_qkv, b_qkv, w_o, b_o, ln_cross, w_qc, b_qc, w_oc, b_oc, ln_mlp, w_fc1, b_fc1, w_fc2, b_fc2, ln_final, w_out):
        num_layers = k_cache.shape[0]
        batch_rows = k_cache.shape[1]
        context = k_cache.shape[2]
        head_dim = k_cache.shape[4]
        positions = jnp.arange(context)
        write_mask = (positions[None, :] == seq_lens[:, None])[:, :, None, None]
        valid_mask = (positions[None, :] <= seq_lens[:, None])[:, None, :]
        residual = tokens.astype(jnp.float32)
        new_keys = []
        new_values = []
        for layer_idx in range(num_layers):
            normed = layer_norm(residual, ln_attn[layer_idx])
            qkv_heads = (jnp.einsum('bw,wcn->bcn', normed, w_qkv[layer_idx], preferred_element_type=jnp.float32) + b_qkv[layer_idx]).astype(jnp.bfloat16).reshape(batch_rows, 3, -1, head_dim)
            key_cache = jnp.where(write_mask, qkv_heads[:, 1][:, None], k_cache[layer_idx])
            value_cache = jnp.where(write_mask, qkv_heads[:, 2][:, None], v_cache[layer_idx])
            attn_out = attend(qkv_heads[:, 0], key_cache, value_cache, valid_mask)
            partial_sum = jnp.dot(attn_out, w_o[layer_idx], preferred_element_type=jnp.float32).astype(jnp.bfloat16)
            residual = residual + lax.psum(partial_sum, 'tp').astype(jnp.float32) + b_o[layer_idx]
            normed = layer_norm(residual, ln_cross[layer_idx])
            cross_query = (jnp.dot(normed, w_qc[layer_idx], preferred_element_type=jnp.float32) + b_qc[layer_idx]).astype(jnp.bfloat16).reshape(batch_rows, -1, head_dim)
            cross_out = attend(cross_query, mem_k[layer_idx], mem_v[layer_idx], True)
            partial_sum = jnp.dot(cross_out, w_oc[layer_idx], preferred_element_type=jnp.float32).astype(jnp.bfloat16)
            residual = residual + lax.psum(partial_sum, 'tp').astype(jnp.float32) + b_oc[layer_idx]
            normed = layer_norm(residual, ln_mlp[layer_idx])
            hidden = jax.nn.gelu(jnp.dot(normed, w_fc1[layer_idx], preferred_element_type=jnp.float32) + b_fc1[layer_idx], approximate=False).astype(jnp.bfloat16)
            partial_sum = jnp.dot(hidden, w_fc2[layer_idx], preferred_element_type=jnp.float32).astype(jnp.bfloat16)
            residual = residual + lax.psum(partial_sum, 'tp').astype(jnp.float32) + b_fc2[layer_idx]
            new_keys.append(key_cache)
            new_values.append(value_cache)
        logits = jnp.dot(layer_norm(residual, ln_final), w_out, preferred_element_type=jnp.float32)
        row_max = lax.pmax(jnp.max(logits, axis=-1, keepdims=True), 'tp')
        shifted = logits - row_max
        exp_sum = lax.psum(jnp.sum(jnp.exp(shifted), axis=-1, keepdims=True), 'tp')
        return shifted - jnp.log(exp_sum), jnp.stack(new_keys), jnp.stack(new_values)

    return jax.shard_map(local_step, mesh=mesh, in_specs=in_specs, out_specs=out_specs, check_vma=False)
```

profile of v0, /device:TPU:0, one launch (start us, length us, event | category | flops | bytes accessed | tf_op | source)
XLA Modules:
  0.0 308.7 jit_solution(12061532663800739773)
XLA Ops:
  12.5 1.3 fusion.82
  14.7 5.3 %multiply_reduce_fusion.3 = f32[256,2,76]{0,1,2:T(2,128)S(1)} fusion(f32[256,2,64]{0,2,1:T(8,128)S(1)} %get-tuple-element.20, pred[256,76]{0,1:T(8,128)(4,1)S(1)} %get-tuple-element.50, bf16[2,256,76,2,64]{1,4,3,2,0:T(8,128)(2,1)} %param.25, bf16[256,2,64]{0,2,1:T(8,128)(2,1)S(1)} %get-tuple-element.19), kind=kLoop, calls=%fused_computation.23 | loop fusion | flops 9922560 | bytes 5352448 | tf_op jit(solution)/shard_map/bhd,bjhd->bhj/dot_general | solution.py:15
  20.6 4.1 %multiply_reduce_fusion.2 = bf16[256,2,64]{0,2,1:T(8,128)(2,1)S(1)} fusion(f32[256,2,76]{0,1,2:T(2,128)S(1)} %fusion.200, pred[256,76]{0,1:T(8,128)(4,1)S(1)} %get-tuple-element.50, bf16[2,256,76,2,64]{1,4,3,2,0:T(8,128)(2,1)} %param.26, bf16[256,2,64]{0,2,1:T(8,128)(2,1)S(1)} %get-tuple-element.18), kind=kLoop, calls=%fused_computation.22 | loop fusion | flops 9928704 | bytes 5286912 | tf_op jit(solution)/shard_map/bhj,bjhd->bhd/dot_general | solution.py:18
  26.3 29.1 %all-reduce.7.cloned.1.call-done = bf16[256,512]{1,0:T(8,128)(2,1)} async-done(((bf16[256,512]{1,0:T(8,128)(2,1)}), bf16[256,512]{1,0:T(8,128)(2,1)}) %all-reduce.7.cloned.1.call-update) | async-done | bytes 262160 | tf_op jit(solution)/shard_map/psum | solution.py:49
  59.1 8.0 %fusion.10 = f32[256,2,1,256]{3,2,1,0:T(1,128)S(1)} fusion(bf16[256,2,64,1]{2,3,1,0:T(2,128)(2,1)S(1)} %copy.45, bf16[2,256,256,2,64]{2,4,3,1,0:T(8,128)(2,1)} %param.27), kind=kOutput, calls=%fused_computation.10 | convolution fusion | flops 16777216 | bytes 17367040 | tf_op jit(solution)/shard_map/bhd,bjhd->bhj/dot_general | solution.py:15
  67.4 10.3 %fusion.8 = bf16[256,2,1,64]{3,2,1,0:T(2,128)(2,1)S(1)} fusion(bf16[2,256,256,2,64]{2,4,3,1,0:T(8,128)(2,1)} %param.28, bf16[256,2,256,1]{2,0,1,3:T(8,128)(2,1)S(1)} %fusion.28), kind=kOutput, calls=%fused_computation.8 | convolution fusion | flops 16777216 | bytes 17104896 | tf_op jit(solution)/shard_map/bhj,bjhd->bhd/dot_general | solution.py:18
  78.9 26.7 %all-reduce.9.cloned.1.call-done = bf16[256,512]{1,0:T(8,128)(2,1)} async-done(((bf16[256,512]{1,0:T(8,128)(2,1)}), bf16[256,512]{1,0:T(8,128)(2,1)}) %all-reduce.9.cloned.1.call-update) | async-done | bytes 262160 | tf_op jit(solution)/shard_map/psum | solution.py:54
  106.9 3.6 %convolution_convert_fusion.3 = bf16[256,512]{1,0:T(8,128)(2,1)} fusion(bf16[2,512,512]{2,1,0:T(8,128)(2,1)} %param.42, bf16[2,512,512]{2,1,0:T(8,128)(2,1)} %param.40, f32[256,512]{1,0:T(8,128)S(1)} %get-tuple-element.8, f32[512]{0:T(512)S(1)} %bitcast.228, f32[512]{0:T(512)S(1)} %bitcast.233, f32[512]{0:T(512)S(1)} %bitcast.234, ...), kind=kOutput, calls=%fused_computation.49 | convolution fusion | flops 277872640 | bytes 1843200 | tf_op jit(solution)/shard_map/dot_general | solution.py:57
  110.8 26.5 %all-reduce.11.cloned.1.call-done = bf16[256,512]{1,0:T(8,128)(2,1)} async-done(((bf16[256,512]{1,0:T(8,128)(2,1)}), bf16[256,512]{1,0:T(8,128)(2,1)}) %all-reduce.11.cloned.1.call-update) | async-done | bytes 262160 | tf_op jit(solution)/shard_map/psum | solution.py:58
  141.2 5.3 %multiply_reduce_fusion.1 = f32[256,2,76]{0,1,2:T(2,128)S(1)} fusion(f32[256,2,64]{0,2,1:T(8,128)S(1)} %get-tuple-element.17, pred[256,76]{0,1:T(8,128)(4,1)S(1)} %get-tuple-element.50, bf16[2,256,76,2,64]{1,4,3,2,0:T(8,128)(2,1)} %param.25, bf16[256,2,64]{0,2,1:T(8,128)(2,1)S(1)} %get-tuple-element.16), kind=kLoop, calls=%fused_computation.21 | loop fusion | flops 9922560 | bytes 5352448 | tf_op jit(solution)/shard_map/bhd,bjhd->bhj/dot_general | solution.py:15
  147.0 4.4 %multiply_reduce_fusion = bf16[256,2,64]{0,2,1:T(8,128)(2,1)S(1)} fusion(f32[256,2,76]{0,1,2:T(2,128)S(1)} %fusion.201, pred[256,76]{0,1:T(8,128)(4,1)S(1)} %get-tuple-element.50, bf16[2,256,76,2,64]{1,4,3,2,0:T(8,128)(2,1)} %param.26, bf16[256,2,64]{0,2,1:T(8,128)(2,1)S(1)} %get-tuple-element.15), kind=kLoop, calls=%fused_computation.20 | loop fusion | flops 9928704 | bytes 5286912 | tf_op jit(solution)/shard_map/bhj,bjhd->bhd/dot_general | solution.py:18
  152.7 26.4 %all-reduce.13.cloned.1.call-done = bf16[256,512]{1,0:T(8,128)(2,1)} async-done(((bf16[256,512]{1,0:T(8,128)(2,1)}), bf16[256,512]{1,0:T(8,128)(2,1)}) %all-reduce.13.cloned.1.call-update) | async-done | bytes 262160 | tf_op jit(solution)/shard_map/psum | solution.py:49
  181.0 8.0 %fusion.6 = f32[256,2,1,256]{3,2,1,0:T(1,128)S(1)} fusion(bf16[256,2,64,1]{2,3,1,0:T(2,128)(2,1)S(1)} %copy.60, bf16[2,256,256,2,64]{2,4,3,1,0:T(8,128)(2,1)} %param.27), kind=kOutput, calls=%fused_computation.6 | convolution fusion | flops 16777216 | bytes 17367040 | tf_op jit(solution)/shard_map/bhd,bjhd->bhj/dot_general | solution.py:15
  189.3 10.2 %fusion.4 = bf16[256,2,1,64]{3,2,1,0:T(2,128)(2,1)S(1)} fusion(bf16[2,256,256,2,64]{2,4,3,1,0:T(8,128)(2,1)} %param.28, bf16[256,2,256,1]{2,0,1,3:T(8,128)(2,1)S(1)} %fusion.29), kind=kOutput, calls=%fused_computation.4 | convolution fusion | flops 16777216 | bytes 17104896 | tf_op jit(solution)/shard_map/bhj,bjhd->bhd/dot_general | solution.py:18
  200.9 15.0 %broadcast_select_fusion.1 = (bf16[1,256,76,2,64]{1,4,3,2,0:T(8,128)(2,1)}, bf16[1,256,76,2,64]{1,4,3,2,0:T(8,128)(2,1)}, bf16[1,256,76,2,64]{1,4,3,2,0:T(8,128)(2,1)}, bf16[1,256,76,2,64]{1,4,3,2,0:T(8,128)(2,1)}) fusion(pred[256,76]{0,1:T(8,128)(4,1)S(1)} %get-tuple-element.50, bf16[2,256,76,2,64]{1,4,3,2,0:T(8,128)(2,1)} %param.26, ...), kind=kLoop, calls=%fused_computation.33 | loop fusion | flops 9961472 | bytes 40127488 | tf_op jit(solution)/shard_map/jit(_where)/select_n | solution.py:46
  215.9 11.4 %all-reduce.15.cloned.1.call-done = bf16[256,512]{1,0:T(8,128)(2,1)} async-done(((bf16[256,512]{1,0:T(8,128)(2,1)}), bf16[256,512]{1,0:T(8,128)(2,1)}) %all-reduce.15.cloned.1.call-update) | async-done | bytes 262160 | tf_op jit(solution)/shard_map/psum | solution.py:54
  228.7 3.6 %convolution_convert_fusion = bf16[256,512]{1,0:T(8,128)(2,1)} fusion(bf16[2,512,512]{2,1,0:T(8,128)(2,1)} %param.42, bf16[2,512,512]{2,1,0:T(8,128)(2,1)} %param.40, f32[256,512]{1,0:T(8,128)S(1)} %get-tuple-element.4, f32[512]{0:T(512)S(1)} %bitcast.227, f32[512]{0:T(512)S(1)} %bitcast.230, f32[512]{0:T(512)S(1)} %bitcast.229, ...), kind=kOutput, calls=%fused_computation.46 | convolution fusion | flops 277872640 | bytes 1843200 | tf_op jit(solution)/shard_map/dot_general | solution.py:57
  232.3 14.9 %pad_maximum_fusion = (bf16[2,256,76,2,64]{1,4,3,2,0:T(8,128)(2,1)}, bf16[2,256,76,2,64]{1,4,3,2,0:T(8,128)(2,1)}) fusion(bf16[1,256,76,2,64]{1,4,3,2,0:T(8,128)(2,1)} %get-tuple-element.21, bf16[1,256,76,2,64]{1,4,3,2,0:T(8,128)(2,1)} %get-tuple-element.22, bf16[1,256,76,2,64]{1,4,3,2,0:T(8,128)(2,1)} %get-tuple-element.10, ...), kind=kLoop, calls=%fused_computation.18 | loop fusion | flops 9961472 | bytes 39845888 | tf_op jit(solution)/shard_map/stack | solution.py:65
  247.2 11.9 %all-reduce.17.cloned.1.call-done = bf16[256,512]{1,0:T(8,128)(2,1)} async-done(((bf16[256,512]{1,0:T(8,128)(2,1)}), bf16[256,512]{1,0:T(8,128)(2,1)}) %all-reduce.17.cloned.1.call-update) | async-done | bytes 262160 | tf_op jit(solution)/shard_map/psum | solution.py:58
  261.3 13.1 %fusion.288 = (f32[256]{0:T(256)S(1)}, f32[256,12352]{0,1:T(8,128)}) fusion(bf16[512,12352]{0,1:T(8,128)(2,1)} %param.45, f32[512]{0:T(512)S(1)} %bitcast.213, f32[512]{0:T(512)S(1)} %bitcast.212, f32[256]{0:T(256)S(1)} %add_rsqrt_fusion, f32[256]{0:T(256)S(1)} %broadcast_multiply_fusion, f32[512]{0:T(512)S(1)} %bitcast.205, ...), kind=kOutput, calls=%fused_computation.371 | convolution fusion | flops 3242213120 | bytes 26092544 | tf_op jit(solution)/shard_map/dot_general | solution.py:61
  274.4 5.7 %pmax.7 = f32[256]{0:T(256)S(1)} all-reduce(f32[256]{0:T(256)S(1)} %get-tuple-element.51), channel_id=1, replica_groups=mesh['dp'=2,'tp'=4] {'tp'}, use_global_device_ids=true, to_apply=%region_29.30 | all-reduce | flops 256 | bytes 2048 | tf_op jit(solution)/shard_map/pmax | solution.py:62
  280.1 5.8 %exponential_reduce_fusion = f32[256]{0:T(256)S(1)} fusion(f32[256,12352]{0,1:T(8,128)} %get-tuple-element.52, f32[256]{0:T(256)S(1)} %pmax.7), kind=kLoop, calls=%fused_computation.16 | loop fusion | flops 6323968 | bytes 12650496 | tf_op jit(solution)/shard_map/reduce_sum | solution.py:64
  285.9 5.8 %psum.55 = f32[256,1]{0,1:T(1,128)S(1)} all-reduce(f32[256,1]{0,1:T(1,128)S(1)} %bitcast.226), channel_id=1, replica_groups=mesh['dp'=2,'tp'=4] {'tp'}, use_global_device_ids=true, to_apply=%region_31.32 | all-reduce | flops 256 | bytes 2048 | tf_op jit(solution)/shard_map/psum | solution.py:64
  291.7 10.2 %subtract_subtract_fusion = f32[256,12352]{0,1:T(8,128)} fusion(f32[256,12352]{0,1:T(8,128)} %get-tuple-element.52, f32[256]{0:T(256)S(1)} %bitcast.225, f32[256]{0:T(256)S(1)} %pmax.7), kind=kLoop, calls=%fused_computation.17 | loop fusion | flops 6324224 | bytes 25298944 | tf_op jit(solution)/shard_map/sub | solution.py:65
  (108 shorter events, 27.6 us)
Async XLA Ops:
  7.2 48.2 %copy-start = (bf16[256,512]{1,0:T(8,128)(2,1)S(1)}, bf16[256,512]{1,0:T(8,128)(2,1)}, u32[]{:S(2)}) copy-start(bf16[256,512]{1,0:T(8,128)(2,1)} %param.23) | copy-start | bytes 786436
  7.2 17.6 %copy-start.3 = (bf16[2,128,512]{2,1,0:T(8,128)(2,1)S(1)}, bf16[2,128,512]{2,1,0:T(8,128)(2,1)}, u32[]{:S(2)}) copy-start(bf16[2,128,512]{2,1,0:T(8,128)(2,1)} %param.32) | copy-start | bytes 786436
  7.2 18.8 %copy-start.7 = (f32[2,512]{1,0:T(2,128)S(1)}, f32[2,512]{1,0:T(2,128)}, u32[]{:S(2)}) copy-start(f32[2,512]{1,0:T(2,128)} %param.33) | copy-start | bytes 12292
  7.2 18.8 %copy-start.5 = (f32[2,2,512]{2,1,0:T(2,128)S(1)}, f32[2,2,512]{2,1,0:T(2,128)}, u32[]{:S(2)}) copy-start(f32[2,2,512]{2,1,0:T(2,128)} %param.34) | copy-start | bytes 24580
  7.2 18.8 %copy-start.8 = (f32[2,512]{1,0:T(2,128)S(1)}, f32[2,512]{1,0:T(2,128)}, u32[]{:S(2)}) copy-start(f32[2,512]{1,0:T(2,128)} %param.38) | copy-start | bytes 12292
  7.2 18.8 %copy-start.6 = (f32[2,2,512]{2,1,0:T(2,128)S(1)}, f32[2,2,512]{2,1,0:T(2,128)}, u32[]{:S(2)}) copy-start(f32[2,2,512]{2,1,0:T(2,128)} %param.39) | copy-start | bytes 24580
  7.2 19.0 %copy-start.12 = (f32[2,128]{1,0:T(2,128)S(1)}, f32[2,128]{1,0:T(2,128)}, u32[]{:S(2)}) copy-start(f32[2,128]{1,0:T(2,128)} %param.36) | copy-start | bytes 3076
  7.2 50.4 %copy-start.13 = (bf16[2,512,128]{2,1,0:T(8,128)(2,1)S(1)}, bf16[2,512,128]{2,1,0:T(8,128)(2,1)}, u32[]{:S(2)}) copy-start(bf16[2,512,128]{2,1,0:T(8,128)(2,1)} %param.35) | copy-start | bytes 786436
  7.2 48.1 %all-reduce.7.cloned.1.call-start = ((), (), s32[]{:S(2)}) async-start(), calls=%async_computation | async-start | bytes 524288 | tf_op jit(solution)/shard_map/psum | solution.py:49
  25.7 79.8 %all-reduce.9.cloned.1.call-start = ((), (), s32[]{:S(2)}) async-start(), calls=%async_computation.1 | async-start | bytes 524288 | tf_op jit(solution)/shard_map/psum | solution.py:54
  67.4 10.4 %copy-start.4 = (bf16[2,128,512]{2,1,0:T(8,128)(2,1)S(1)}, bf16[2,128,512]{2,1,0:T(8,128)(2,1)}, u32[]{:S(2)}) copy-start(bf16[2,128,512]{2,1,0:T(8,128)(2,1)} %param.37) | copy-start | bytes 786436
  67.4 11.4 %copy-start.9 = (f32[2,512]{1,0:T(2,128)S(1)}, f32[2,512]{1,0:T(2,128)}, u32[]{:S(2)}) copy-start(f32[2,512]{1,0:T(2,128)} %param.41) | copy-start | bytes 12292
  67.4 38.1 %copy-start.2 = (bf16[256,512]{1,0:T(8,128)(2,1)S(1)}, bf16[256,512]{1,0:T(8,128)(2,1)}, u32[]{:S(2)}) copy-start(bf16[256,512]{1,0:T(8,128)(2,1)} %all-reduce.7.cloned.1.call-done) | copy-start | bytes 786436
  77.7 33.2 %copy-start.10 = (f32[2,512]{1,0:T(2,128)S(1)}, f32[2,512]{1,0:T(2,128)}, u32[]{:S(2)}) copy-start(f32[2,512]{1,0:T(2,128)} %param.43) | copy-start | bytes 12292
  78.8 58.5 %all-reduce.11.cloned.1.call-start = ((), (), s32[]{:S(2)}) async-start(), calls=%async_computation.2 | async-start | bytes 524288 | tf_op jit(solution)/shard_map/psum | solution.py:58
  110.5 42.1 %copy-start.11 = (f32[2,512]{1,0:T(2,128)S(1)}, f32[2,512]{1,0:T(2,128)}, u32[]{:S(2)}) copy-start(f32[2,512]{1,0:T(2,128)} %param.44) | copy-start | bytes 12292
  110.5 68.5 %all-reduce.13.cloned.1.call-start = ((), (), s32[]{:S(2)}) async-start(), calls=%async_computation.3 | async-start | bytes 524288 | tf_op jit(solution)/shard_map/psum | solution.py:49
  137.3 41.8 %copy-start.1 = (bf16[256,512]{1,0:T(8,128)(2,1)S(1)}, bf16[256,512]{1,0:T(8,128)(2,1)}, u32[]{:S(2)}) copy-start(bf16[256,512]{1,0:T(8,128)(2,1)} %all-reduce.11.cloned.1.call-done) | copy-start | bytes 786436
  152.3 75.0 %all-reduce.15.cloned.1.call-start = ((), (), s32[]{:S(2)}) async-start(), calls=%async_computation.4 | async-start | bytes 524288 | tf_op jit(solution)/shard_map/psum | solution.py:54
  200.6 58.5 %all-reduce.17.cloned.1.call-start = ((), (), s32[]{:S(2)}) async-start(), calls=%async_computation.5 | async-start | bytes 524288 | tf_op jit(solution)/shard_map/psum | solution.py:58
Sparse Core Ops, SparseCore 0:
  25.8 29.4 all-reduce.6
  78.9 26.5 all-reduce.8
  110.7 26.5 all-reduce.10
  152.5 26.5 all-reduce.12
  200.7 26.5 all-reduce.14
  232.4 26.5 all-reduce.16
where the time goes:
time: 310 us; the launch traced here: 309 us
  waiting for transfers between devices  132 us (43%)
  other arithmetic  80.7 us (26%)
  matrix products  64.9 us (21%)
  between operations  14.6 us (5%)
  blocking collectives  11.5 us (4%)
  local copies, waits for them, and re-layouts  3.83 us (1%)
    psum x6, waiting for transfers between devices, local_step(): lax.psum(partial_sum, 'tp').astype(jnp.float32)  132 us
    dot_general x2, matrix products, attend(): jnp.einsum('bhj,bjhd->bhd', attn_probs, value_heads, preferred_element_ty...  20.5 us
    dot_general x2, matrix products, attend(): jnp.einsum('bhd,bjhd->bhj', query_heads, key_heads, preferred_element_typ...  16.1 us
    select_n x1, other arithmetic, local_step(): jnp.where(write_mask, qkv_heads[:, 2][:, None], v_cache[layer_idx])  15 us
    another operation x1, other arithmetic, local_step(): jnp.stack(new_keys)  14.9 us
    dot_general x1, matrix products, local_step(): jnp.dot(layer_norm(residual, ln_final), w_out, preferred_element_type=jnp...  13.1 us
    dot_general x2, other arithmetic, attend(): jnp.einsum('bhd,bjhd->bhj', query_heads, key_heads, preferred_element_typ...  10.6 us
    sub x1, other arithmetic, local_step(): shifted - jnp.log(exp_sum)  10.2 us
  transfers between devices with their start and end apart: 6, of which 6 were waited for; matrix products, arithmetic and copies ran while one was open for 10% of the time, Pallas kernels for 0%

commit v1 on v0

v1 whole, which is shorter than its diff:
```python
import functools
import math

import jax
import jax.numpy as jnp
from jax import lax
from jax.experimental import pallas as pl
from jax.experimental.pallas import tpu as pltpu
from jax.sharding import PartitionSpec as P

BF = jnp.bfloat16
F32 = jnp.float32
MESH = pl.DeviceIdType.MESH
RING = 12
CHUNK = 16
HEAD_CHUNKS = 4
LANES = 128
HD = 64
ROWS = 256
WIDTH = 512


def dot(a, b):
    return jnp.dot(a, b, preferred_element_type=F32)


def dot_nt(a, b):
    return lax.dot_general(a, b, (((1,), (1,)), ((), ())), preferred_element_type=F32)


def norm(x, gain, shift):
    mean = jnp.mean(x, axis=-1, keepdims=True)
    centred = x - mean
    var = jnp.mean(centred * centred, axis=-1, keepdims=True)
    return (centred * lax.rsqrt(var + 1e-5) * gain + shift).astype(BF)


def fold(x8, op):
    x8 = op(x8, pltpu.roll(x8, 4, 0))
    return op(x8, pltpu.roll(x8, 2, 0))


def decode_kernel(tok, lens, kc, vc, mk, mv, lna, wqkv, bqkv, wo, bo, lnc, wqc, bqc, woc, boc, lnm, w1, b1, w2, b2, lnf, wout,
                  xn_out, lse_out, kn_out, vn_out,
                  mkb, mvb, ckb, cvb, wqkvb, wob, wqcb, w1b, w2b, woutb, b1x,
                  xown, xn0, xng, obuf, orecv, xsend, xrecv, q2s, qbm, pm, racc, qT, kT, vT, ss, msb, msr,
                  lw_sem, rws_sem, rwr_sem, c_sem, mk_sem, mv_sem, wo_sem, es, er, xs, xr, gs, gr, ls, lr):
    L = kc.shape[0]
    ctx = kc.shape[1]
    me = lax.axis_index('tp')
    c = lax.rem(me, 2)
    partner = me + 1 - 2 * c
    peer = lax.rem(me + 2, 4)
    own = pl.multiple_of(c * HD, HD)
    oth = pl.multiple_of((1 - c) * HD, HD)

    def seq_chunk(n):
        layer = n // 16
        within = n % 16
        half = within // 8
        sub = (within % 8) // 4
        grp = sub + (1 - 2 * sub) * (1 - c)
        seq = half * LANES + grp * HD + (within % 4) * CHUNK
        return layer, seq

    def mem_copies(n):
        layer, seq = seq_chunk(n)
        slot = n % RING
        return (pltpu.make_async_copy(mk.at[layer, pl.ds(seq, CHUNK)], mkb.at[slot], mk_sem.at[slot]),
                pltpu.make_async_copy(mv.at[layer, pl.ds(seq, CHUNK)], mvb.at[slot], mv_sem.at[slot]))

    def cache_copies(l):
        return (pltpu.make_async_copy(kc.at[l], ckb, c_sem.at[0]),
                pltpu.make_async_copy(vc.at[l], cvb, c_sem.at[1]))

    def weight_copies(l):
        pairs = ((wqkv.at[l], wqkvb.at[l]), (wo.at[l], wob.at[l, 0, 0]), (wqc.at[l], wqcb.at[l]),
                 (woc.at[l], wob.at[l, 1, 0]), (w1.at[l], w1b.at[l, 0]), (w2.at[l], w2b.at[l, 0]))
        return [pltpu.make_async_copy(s, d, lw_sem.at[l, i]) for i, (s, d) in enumerate(pairs)]

    def shared_copies(l):
        pairs = [(wo.at[l], wob.at[l, 0, 1]), (woc.at[l], wob.at[l, 1, 1]), (w1.at[l], w1b.at[l, 1]), (w2.at[l], w2b.at[l, 1])]
        if l == 0:
            pairs.append((b1, b1x))
        return [pltpu.make_async_remote_copy(s, d, rws_sem.at[l, i], rwr_sem.at[l, i], device_id={'tp': partner}, device_id_type=MESH)
                for i, (s, d) in enumerate(pairs)]

    def head_copies():
        rows = woutb.shape[1]
        return [pltpu.make_async_copy(wout.at[pl.ds(i * rows, rows)], woutb.at[i], wo_sem.at[i]) for i in range(HEAD_CHUNKS)]

    weights = [weight_copies(l) for l in range(L)]
    shared = [shared_copies(l) for l in range(L)]
    caches = [cache_copies(l) for l in range(L)]
    heads = head_copies()

    weights[0][0].start()
    caches[0][0].start()
    caches[0][1].start()
    for w in weights[0][1:]:
        w.start()
    for n in range(RING):
        for m in mem_copies(n):
            m.start()

    barrier = pltpu.get_barrier_semaphore()
    for d in range(1, 4):
        pl.semaphore_signal(barrier, inc=1, device_id={'tp': lax.rem(me + d, 4)}, device_id_type=MESH)
    pl.semaphore_wait(barrier, 3)
    for l in range(L):
        for s in shared[l]:
            s.start()
    for w in weights[1]:
        w.start()

    row = lax.broadcasted_iota(jnp.int32, (32, 2048), 0)
    lane = lax.broadcasted_iota(jnp.int32, (32, 2048), 1)
    qbm[...] = jnp.where(lane // HD == row, 1.0, 0.0).astype(BF)
    pm[...] = jnp.zeros_like(pm)
    for h in range(2):
        xown[h] = tok[pl.ds(pl.multiple_of(h * LANES + own, HD), HD), :].astype(F32)

    def self_attention(l, hf):
        lanes = pl.ds(hf * LANES, LANES)
        if l == 0:
            xn = norm(tok[hf * LANES:(hf + 1) * LANES, :].astype(F32), lna[0, 0:1], lna[0, 1:2])
            if hf == 0:
                weights[0][0].wait()
        else:
            if hf == 0:
                weights[1][0].wait()
            gathers[(l - 1, 1, hf)].wait()
            xn = xng[l - 1, 1, hf]
        for i, ref in enumerate((qT, kT, vT)):
            y = (dot(xn, wqkvb[l, i]) + bqkv[i, l:l + 1]).astype(BF)
            ref[...] = y.astype(F32).T
        kn_out[l, :, lanes] = kT[...].astype(BF)
        vn_out[l, :, lanes] = vT[...].astype(BF)
        if hf == 0:
            caches[l][0].wait()

        def k_body(t, _):
            blk = ckb[pl.ds(t * 4, 4), :, lanes].astype(F32) * qT[...][None]
            ss[pl.ds(pl.multiple_of(t * 8, 8), 8), :] = jnp.sum(blk.reshape(8, HD, LANES), axis=1) * 0.125
            return 0

        lax.fori_loop(0, ctx // 4, k_body, 0)
        snew = jnp.sum((qT[...] * kT[...]).reshape(2, HD, LANES), axis=1) * 0.125
        snew = jnp.concatenate([snew] * 4, axis=0)
        s = ss[...].reshape(ctx // 4, 8, LANES)
        pos = (lax.broadcasted_iota(jnp.int32, s.shape, 0) * 4 + lax.broadcasted_iota(jnp.int32, s.shape, 1) // 2)
        ln = lens[0:1, lanes][None]
        fresh = pos == ln
        s = jnp.where(fresh, snew[None], jnp.where(pos < ln, s, -1e30))
        m8 = fold(jnp.max(s, axis=0), jnp.maximum)
        p = jnp.exp(s - m8[None])
        l8 = fold(jnp.sum(p, axis=0), jnp.add)
        p = (p / l8[None]).astype(BF).astype(F32)
        pn = fold(jnp.sum(jnp.where(fresh, p, 0.0), axis=0), jnp.add)
        ss[...] = jnp.where(fresh, 0.0, p).reshape(ctx * 2, LANES)
        if hf == 0:
            caches[l][1].wait()

        def v_body(t, acc):
            blk = cvb[pl.ds(t * 4, 4), :, lanes].astype(F32)
            pr = ss[pl.ds(pl.multiple_of(t * 8, 8), 8), :]
            acc = list(acc)
            for j in range(4):
                for h in range(2):
                    acc[h] = acc[h] + blk[j, h * HD:(h + 1) * HD] * pr[2 * j + h:2 * j + h + 1]
            return tuple(acc)

        acc = tuple(vT[h * HD:(h + 1) * HD, :] * pn[h:h + 1] for h in range(2))
        acc = lax.fori_loop(0, ctx // 4, v_body, acc)
        oT = jnp.concatenate(acc, axis=0).astype(BF).astype(F32)
        obuf[l, 0, hf] = oT.T.astype(BF)
        send_o(l, 0, hf)

    sent = []
    swaps, crosses, gathers = {}, {}, {}

    def remote(src, dst, ssem, rsem, dev):
        cp = pltpu.make_async_remote_copy(src, dst, ssem, rsem, device_id={'tp': dev}, device_id_type=MESH)
        cp.start()
        return cp

    def send_o(l, k, hf):
        swaps[(l, k, hf)] = remote(obuf.at[l, k, hf, pl.ds(oth, HD)], orecv.at[l, k, hf], es.at[l, k, hf], er.at[l, k, hf], partner)

    def send_x(l, k, hf, part):
        xsend[l, k, hf] = part.astype(BF)
        crosses[(l, k, hf)] = remote(xsend.at[l, k, hf], xrecv.at[l, k, hf], xs.at[l, k, hf], xr.at[l, k, hf], peer)

    def project(l, k, hf):
        if hf == 0:
            weights[l][1 if k == 0 else 3].wait()
            shared[l][k].wait()
        swaps[(l, k, hf)].wait()
        part = dot(obuf[l, k, hf, pl.ds(own, HD)], wob[l, k, 0]) + dot(orecv[l, k, hf], wob[l, k, 1])
        send_x(l, k, hf, part)

    def add_up(l, k, hf, bias):
        crosses[(l, k, hf)].wait()
        x = xown[hf] + (xsend[l, k, hf].astype(F32) + xrecv[l, k, hf].astype(F32)) + bias
        xown[hf] = x
        return x

    def gather(l, k, hf, xn):
        rows = pl.ds(own, HD)
        xng[l, k, hf, rows] = xn
        gathers[(l, k, hf)] = remote(xng.at[l, k, hf, rows], xng.at[l, k, hf, rows], gs.at[l, k, hf], gr.at[l, k, hf], partner)

    def finish_self(l, hf):
        x = add_up(l, 0, hf, bo[l:l + 1])
        gather(l, 0, hf, norm(x, lnc[l, 0:1], lnc[l, 1:2]))

    def start_cross(l, hf):
        if hf == 0:
            weights[l][2].wait()
        gathers[(l, 0, hf)].wait()
        q = (dot(xng[l, 0, hf], wqcb[l]) + bqc[l:l + 1]).astype(BF)
        dup = jnp.where(lax.broadcasted_iota(jnp.int32, (ROWS, LANES), 0) // 2 == lax.broadcasted_iota(jnp.int32, (ROWS, LANES), 1), 1.0, 0.0).astype(BF)
        q2s[hf] = dot(dup, q).astype(BF)

    def cross_part(l, hf, sub):
        base = l * 16 + hf * 8 + sub * 4
        grp = sub + (1 - 2 * sub) * (1 - c)
        lane_id = lax.broadcasted_iota(jnp.int32, (LANES, LANES), 1)
        head_id = lax.broadcasted_iota(jnp.int32, (LANES, LANES), 0) // HD

        def body(t, _):
            n = base + t
            slot = lax.rem(n, RING)
            for m in mem_copies(n):
                m.wait()
            q = q2s[hf, pl.ds(pl.multiple_of(grp * LANES + t * 32, 32), 32), :]
            qbd = jnp.concatenate([q] * 16, axis=1) * qbm[...]
            s = dot(qbd, mkb[slot].reshape(CHUNK * LANES, ROWS)) * 0.125
            e = jnp.exp(s - jnp.max(s, axis=-1, keepdims=True))
            p = e / jnp.sum(e, axis=-1, keepdims=True)
            pm[pl.ds(pl.multiple_of(t * 32, 32), 32), :] = p.astype(BF)
            out = dot_nt(mvb[slot].reshape(CHUNK * LANES, ROWS), pm[...])
            r = racc[...]
            for i in range(CHUNK):
                r = jnp.where(lane_id == t * 32 + 2 * i + head_id, out[i * LANES:(i + 1) * LANES], r)
            racc[...] = r

            @pl.when(n + RING < 16 * L)
            def _():
                for m in mem_copies(n + RING):
                    m.start()
            return 0

        lax.fori_loop(0, 4, body, 0)
        r = jnp.where(lax.rem(lane_id, 2) == head_id, racc[...], 0.0).astype(BF)
        sel = jnp.where(lax.broadcasted_iota(jnp.int32, (HD, LANES), 1) // 2 == lax.broadcasted_iota(jnp.int32, (HD, LANES), 0), 1.0, 0.0).astype(BF)
        obuf[l, 1, hf, pl.ds(pl.multiple_of(grp * HD, HD), HD)] = dot_nt(sel, r).astype(BF)
        if sub == 0:
            send_o(l, 1, hf)

    def mlp(l, hf):
        x = add_up(l, 1, hf, boc[l:l + 1])
        xn = norm(x, lnm[l, 0:1], lnm[l, 1:2])
        if hf == 0:
            weights[l][4].wait()
            weights[l][5].wait()
            shared[l][2].wait()
            shared[l][3].wait()
            if l == 0:
                shared[0][4].wait()
        part = None
        for k in range(2):
            a = dot(xn, w1b[l, k]) + (b1 if k == 0 else b1x)[l:l + 1]
            a = (0.5 * a * (1.0 + lax.erf(a * math.sqrt(0.5)))).astype(BF)
            d = dot(a, w2b[l, k])
            part = d if part is None else part + d
        send_x(l, 2, hf, part)

    def finish_mlp(l, hf):
        x = add_up(l, 2, hf, b2[l:l + 1])
        last = l == L - 1
        params = lnf if last else lna.at[l + 1]
        gather(l, 1, hf, norm(x, params[0:1], params[1:2]))

    for l in range(L):
        self_attention(l, 0)
        self_attention(l, 1)
        if l == 0:
            for cp in caches[1]:
                cp.start()
            for cp in heads:
                cp.start()
        project(l, 0, 0)
        project(l, 0, 1)
        finish_self(l, 0)
        finish_self(l, 1)
        start_cross(l, 0)
        cross_part(l, 0, 0)
        cross_part(l, 0, 1)
        project(l, 1, 0)
        start_cross(l, 1)
        cross_part(l, 1, 0)
        mlp(l, 0)
        cross_part(l, 1, 1)
        project(l, 1, 1)
        finish_mlp(l, 0)
        mlp(l, 1)
        finish_mlp(l, 1)

    for hf in range(2):
        gathers[(L - 1, 1, hf)].wait()
        xn_out[hf * LANES:(hf + 1) * LANES, :] = xng[L - 1, 1, hf]
    for h in heads:
        h.wait()
    rows = woutb.shape[1]

    def head_body(i, carry):
        m, s = carry
        z = dot_nt(woutb[i], xn_out[...]).reshape(rows // 8, 8, ROWS)
        m2 = jnp.maximum(m, jnp.max(z, axis=0))
        s = s * jnp.exp(m - m2) + jnp.sum(jnp.exp(z - m2[None]), axis=0)
        return m2, s

    m, s = lax.fori_loop(0, HEAD_CHUNKS, head_body, (jnp.full((8, ROWS), -jnp.inf, F32), jnp.zeros((8, ROWS), F32)))
    top = jnp.max(m, axis=0, keepdims=True)
    tot = jnp.sum(s * jnp.exp(m - top), axis=0, keepdims=True)
    msb[0:8] = jnp.broadcast_to(top, (8, ROWS))
    msb[8:16] = jnp.broadcast_to(tot, (8, ROWS))
    outs = [remote(msb, msr.at[d - 1], ls.at[d - 1], lr.at[d - 1], lax.rem(me + d, 4)) for d in range(1, 4)]
    for o in outs:
        o.wait()
    big = jnp.maximum(jnp.maximum(msb[0:8], msr[0, 0:8]), jnp.maximum(msr[1, 0:8], msr[2, 0:8]))
    total = msb[8:16] * jnp.exp(msb[0:8] - big)
    for d in range(3):
        total = total + msr[d, 8:16] * jnp.exp(msr[d, 0:8] - big)
    lse_out[...] = big + jnp.log(total)


def decode(args):
    (tok, lens, kc, vc, mk, mv, lna, wqkv, bqkv, wo, bo, lnc, wqc, bqc, woc, boc, lnm, w1, b1, w2, b2, lnf, wout) = args
    L, ctx = kc.shape[:2]
    vrows = wout.shape[0] // HEAD_CHUNKS
    V = pltpu.VMEM
    dma = pltpu.SemaphoreType.DMA
    hbm = pl.BlockSpec(memory_space=pl.ANY)
    vm = pl.BlockSpec(memory_space=pltpu.VMEM)
    big = {2, 3, 4, 5, 7, 9, 12, 14, 17, 19, 22}
    return pl.pallas_call(
        decode_kernel,
        out_shape=(jax.ShapeDtypeStruct((ROWS, WIDTH), BF), jax.ShapeDtypeStruct((8, ROWS), F32),
                   jax.ShapeDtypeStruct((L, LANES, ROWS), BF), jax.ShapeDtypeStruct((L, LANES, ROWS), BF)),
        in_specs=[hbm if i in big else vm for i in range(23)],
        out_specs=(vm, vm, vm, vm),
        scratch_shapes=[
            V((RING, CHUNK, LANES, ROWS), BF), V((RING, CHUNK, LANES, ROWS), BF),
            V((ctx, LANES, ROWS), BF), V((ctx, LANES, ROWS), BF),
            V((L, 3, WIDTH, LANES), BF), V((L, 2, 2, LANES, WIDTH), BF), V((L, WIDTH, LANES), BF),
            V((L, 2, WIDTH, WIDTH), BF), V((L, 2, WIDTH, WIDTH), BF), V((HEAD_CHUNKS, vrows, WIDTH), BF), V((L, WIDTH), F32),
            V((2, HD, WIDTH), F32), V((LANES, WIDTH), BF), V((L, 2, 2, LANES, WIDTH), BF),
            V((L, 2, 2, LANES, LANES), BF), V((L, 2, 2, HD, LANES), BF),
            V((L, 3, 2, HD, WIDTH), BF), V((L, 3, 2, HD, WIDTH), BF),
            V((2, ROWS, LANES), BF), V((32, 2048), BF), V((LANES, ROWS), BF), V((LANES, LANES), F32),
            V((LANES, LANES), F32), V((LANES, LANES), F32), V((LANES, LANES), F32), V((ctx * 2, LANES), F32),
            V((16, ROWS), F32), V((3, 16, ROWS), F32),
            dma((L, 6)), dma((L, 5)), dma((L, 5)), dma((2,)), dma((RING,)), dma((RING,)), dma((HEAD_CHUNKS,)),
            dma((L, 2, 2)), dma((L, 2, 2)), dma((L, 3, 2)), dma((L, 3, 2)), dma((L, 2, 2)), dma((L, 2, 2)), dma((3,)), dma((3,)),
        ],
        compiler_params=pltpu.CompilerParams(collective_id=0, has_side_effects=True, vmem_limit_bytes=67043328),
        name='decode',
    )(*args)


def write_kernel(lens, kn, vn, kc, vc, wout, xn, lse, k_out, v_out, logp, *, blk, ctx):
    first = lax.rem(pl.program_id(0) * blk, ctx)
    for src, new, dst in ((kc, kn, k_out), (vc, vn, v_out)):
        for j in range(blk):
            hit = lens[...] == first + j
            dst[j] = jnp.where(hit, new[0], src[j])
    logp[...] = dot_nt(wout[...], xn[...]) - lse[0:1]


def write_out(lens, kn, vn, kc, vc, wout, xn, lse):
    L, ctx = kc.shape[:2]
    steps = 8
    blk = L * ctx // steps
    per = steps // L
    vocab = wout.shape[0]
    rows = -(-vocab // steps // 16) * 16
    whole = lambda a: pl.BlockSpec(a.shape, lambda i: (0,) * a.ndim)
    cache = pl.BlockSpec((blk, LANES, ROWS), lambda i: (i, 0, 0))
    fresh = pl.BlockSpec((1, LANES, ROWS), lambda i: (i // per, 0, 0))
    flat = (L * ctx, LANES, ROWS)
    k, v, logp = pl.pallas_call(
        functools.partial(write_kernel, blk=blk, ctx=ctx),
        grid=(steps,),
        out_shape=(jax.ShapeDtypeStruct(flat, BF), jax.ShapeDtypeStruct(flat, BF), jax.ShapeDtypeStruct((vocab, ROWS), F32)),
        in_specs=[whole(lens), fresh, fresh, cache, cache, pl.BlockSpec((rows, WIDTH), lambda i: (i, 0)), whole(xn), whole(lse)],
        out_specs=(cache, cache, pl.BlockSpec((rows, ROWS), lambda i: (i, 0))),
        name='write',
    )(lens, kn, vn, kc.reshape(flat), vc.reshape(flat), wout, xn, lse)
    return k.reshape(kc.shape), v.reshape(vc.shape), logp


def solution(mesh):
    cache_spec = P(None, 'dp', None, 'tp', None)
    in_specs = (P('dp', None), P('dp'), cache_spec, cache_spec, cache_spec, cache_spec,
                P(), P(None, None, None, 'tp'), P(None, None, 'tp'), P(None, 'tp', None), P(),
                P(), P(None, None, 'tp'), P(None, 'tp'), P(None, 'tp', None), P(),
                P(), P(None, None, 'tp'), P(None, 'tp'), P(None, 'tp', None), P(),
                P(), P(None, 'tp'))
    out_specs = (P('dp', 'tp'), cache_spec, cache_spec)

    def local_step(tokens, seq_lens, k_cache, v_cache, mem_k, mem_v, ln_attn, w_qkv, b_qkv, w_o, b_o, ln_cross, w_qc, b_qc, w_oc, b_oc, ln_mlp, w_fc1, b_fc1, w_fc2, b_fc2, ln_final, w_out):
        L, B, ctx, H, D = k_cache.shape
        M = mem_k.shape[2]
        lens = seq_lens.reshape(1, B)
        kc = k_cache.transpose(0, 2, 3, 4, 1).reshape(L, ctx, H * D, B)
        vc = v_cache.transpose(0, 2, 3, 4, 1).reshape(L, ctx, H * D, B)
        mk = mem_k.transpose(0, 1, 3, 4, 2).reshape(L, B, H * D, M)
        mv = mem_v.transpose(0, 1, 3, 4, 2).reshape(L, B, H * D, M)
        wout = w_out.T
        xn, lse, kn, vn = decode((tokens, lens, kc, vc, mk, mv, ln_attn, w_qkv.transpose(0, 2, 1, 3), b_qkv.transpose(1, 0, 2), w_o, b_o, ln_cross, w_qc, b_qc,
                                  w_oc, b_oc, ln_mlp, w_fc1, b_fc1, w_fc2, b_fc2, ln_final, wout))
        k, v, logp = write_out(lens, kn, vn, kc, vc, wout, xn, lse)
        back = lambda a: a.reshape(L, ctx, H, D, B).transpose(0, 4, 1, 2, 3)
        return logp.T, back(k), back(v)

    return jax.shard_map(local_step, mesh=mesh, in_specs=in_specs, out_specs=out_specs, check_vma=False)
```

time: 310 us -> 125 us (0.40)
  waiting for transfers between devices: 132 us -> 0 us
  Pallas kernels: 0 us -> 124 us
  other arithmetic: 80.7 us -> 0 us
  matrix products: 64.9 us -> 0 us
  between operations: 14.6 us -> 0.65 us
  blocking collectives: 11.5 us -> 0 us
  local copies, waits for them, and re-layouts: 3.83 us -> 0 us
    psum x6 -> x0, waiting for transfers between devices: 132 us -> none  [local_step(): lax.psum(partial_sum, 'tp').astype(jnp.float32)]
    pallas_call x0 -> x2, Pallas kernels: none -> 124 us  [the longest x1 101 us: decode(): pl.pallas_call(decode_kernel, out_shape=(jax.ShapeDtypeStruct((ROWS, WIDT...]
    dot_general x13 -> x0, matrix products: 62.2 us -> none  [the longest x2 20.5 us: attend(): jnp.einsum('bhj,bjhd->bhd', attn_probs, value_heads, preferred_element_ty...]
    reduce_sum x17 -> x0, other arithmetic: 19.3 us -> none  [the longest x7 7.86 us: layer_norm(): mean_val = jnp.mean(hidden, axis=-1, keepdims=True)]
    dot_general x4 -> x0, other arithmetic: 19.1 us -> none  [the longest x2 10.6 us: attend(): jnp.einsum('bhd,bjhd->bhj', query_heads, key_heads, preferred_element_typ...]
    select_n x1 -> x0, other arithmetic: 15 us -> none  [local_step(): jnp.where(write_mask, qkv_heads[:, 2][:, None], v_cache[layer_idx])]
    another operation x1 -> x0, other arithmetic: 14.9 us -> none  [local_step(): jnp.stack(new_keys)]
    sub x1 -> x0, other arithmetic: 10.2 us -> none  [local_step(): shifted - jnp.log(exp_sum)]
  transfers between devices with their start and end apart: 6 -> 0, of which waited for: 6 -> 0; matrix products, arithmetic and copies ran while one was open for 10% -> 0% of each run, Pallas kernels for 0% -> 0%
where the time goes in v1:
time: 125 us
  Pallas kernels  124 us (99%)
    pallas_call x1, Pallas kernels, decode(): pl.pallas_call(decode_kernel, out_shape=(jax.ShapeDtypeStruct((ROWS, WIDT...  101 us
    pallas_call x1, Pallas kernels, write_out(): pl.pallas_call(functools.partial(write_kernel, blk=blk, ctx=ctx), grid=(s...  23.6 us

profile of v1, /device:TPU:0, one launch (start us, length us, event | category | flops | bytes accessed | tf_op | source)
XLA Modules:
  0.0 124.9 jit_solution(9432309879996025228)
XLA Ops:
  0.6 100.7 %decode.1 = (bf16[256,512]{1,0:T(8,128)(2,1)}, f32[8,256]{1,0:T(8,128)}, bf16[2,128,256]{2,1,0:T(8,128)(2,1)}, bf16[2,128,256]{2,1,0:T(8,128)(2,1)}) custom-call(bf16[256,512]{1,0:T(8,128)(2,1)} %tok.1, s32[1,256]{1,0:T(1,128)} %bitcast.36, bf16[2,76,128,256]{3,2,1,0:T(8,128)(2,1)} %bitcast.29, bf16[2,76,128,256]{3,2,1,0:T(8,128)(2,1)} %bitcast.31, ...), custom_call_target="tpu_custom_call" | custom-call | tf_op jit(solution)/shard_map/decode/pallas_call | solution.py:348
  101.3 23.6 %write.1 = (bf16[152,128,256]{2,1,0:T(8,128)(2,1)}, bf16[152,128,256]{2,1,0:T(8,128)(2,1)}, f32[12352,256]{1,0:T(8,128)}) custom-call(s32[1,256]{1,0:T(1,128)} %bitcast.37, bf16[2,128,256]{2,1,0:T(8,128)(2,1)} %get-tuple-element.10.kn, bf16[2,128,256]{2,1,0:T(8,128)(2,1)} %get-tuple-element.11.vn, bf16[152,128,256]{2,1,0:T(8,128)(2,1)} %bitcast.30, ...), custom_call_target="tpu_custom_call" | custom-call | tf_op jit(solution)/shard_map/write/pallas_call | solution.py:393
